TPU v7x, 32 devices: a whole 2x2x4 slice. The times are simulated.
32 devices in a mesh: dp: 8 (over y, x, core), tensor: 4 (over z).
Axes of the slice: x: 2, y: 2, z: 4, core: 2. Of those that a mesh axis runs over, the one named last changes fastest.
Arguments:
- node_features: bfloat16 [8192, 768], P(('dp', 'tensor')), may hold values from -6 to 6
- graph_ids: int32 [64, 128], P('dp'), may hold values from 0 to 5, never falling along the last dimension, each value on 1 to 32 neighbouring positions
- degree: int32 [8192], P(('dp', 'tensor')), may hold values from 0 to 511
- distance: int32 [8192, 128], P('dp'), may hold values from 0 to 511
- out_grad: bfloat16 [8192, 768], P(('dp', 'tensor')), may hold values from -6 to 6
- qkv_weight: bfloat16 [3, 768, 768], P(None, 'tensor'), may hold values from -0.21875 to 0.21875
- qv_bias: float32 [2, 768], P(None, 'tensor'), may hold values from -3 to 3
- out_weight: bfloat16 [768, 768], P('tensor'), may hold values from -0.625 to 0.625
- out_bias: float32 [768], replicated, may hold values from -3 to 3
- norm1_gain: float32 [768], replicated, may hold values from 0.5 to 1.5
- norm1_shift: float32 [768], replicated, may hold values from -2 to 2
- ffn_in_weight: bfloat16 [768, 768], P('tensor'), may hold values from -0.21875 to 0.21875
- ffn_in_bias: float32 [768], P('tensor'), may hold values from -3 to 3
- ffn_out_weight: bfloat16 [768, 768], P('tensor'), may hold values from -0.21875 to 0.21875
- ffn_out_bias: float32 [768], replicated, may hold values from -3 to 3
- norm2_gain: float32 [768], replicated, may hold values from 0.5 to 1.5
- norm2_shift: float32 [768], replicated, may hold values from -2 to 2
- degree_table: bfloat16 [512, 768], replicated, may hold values from -3 to 3
- spatial_table: bfloat16 [32, 512], P('tensor'), may hold values from -4 to 4
Outputs:
- layer_out: bfloat16 [8192, 768], P(('dp', 'tensor'))
- input_grad: bfloat16 [8192, 768], P(('dp', 'tensor'))
- qkv_weight_grad: float32 [3, 768, 768], P(None, 'tensor')
- qv_bias_grad: float32 [2, 768], P(None, 'tensor')
- out_weight_grad: float32 [768, 768], P('tensor')
- out_bias_grad: float32 [768], replicated
- norm1_gain_grad: float32 [768], replicated
- norm1_shift_grad: float32 [768], replicated
- ffn_in_weight_grad: float32 [768, 768], P('tensor')
- ffn_in_bias_grad: float32 [768], P('tensor')
- ffn_out_weight_grad: float32 [768, 768], P('tensor')
- ffn_out_bias_grad: float32 [768], replicated
- norm2_gain_grad: float32 [768], replicated
- norm2_shift_grad: float32 [768], replicated
- degree_table_grad: float32 [512, 768], replicated
- spatial_table_grad: float32 [32, 512], P('tensor')
Inputs may be any that keep to these rules, and one draw needn't show every extreme that they name: `graph_ids`: graph numbers never fall along a packed block; a graph holds at most a quarter of 128 nodes, and in every block some graph holds exactly that many.
All inputs are finite; a program needn't handle non-finite values.
Results may differ from a plain program's by a relative error of at most 0.018.
Values may be sent and summed in bfloat16 or wider, within the bound.
A program may use at most 128 MiB of HBM per device.

v0:
```python
import math
import jax
import jax.numpy as jnp
from jax import lax
from jax.sharding import PartitionSpec as P

norm_eps = 1e-05
masked_score = -1e30


def norm_rows(hidden_rows, gain, shift):
    row_mean = jnp.mean(hidden_rows, axis=1, keepdims=True)
    centered = hidden_rows - row_mean
    variance = jnp.mean(centered * centered, axis=1, keepdims=True)
    inverse = lax.rsqrt(variance + norm_eps)
    normed = centered * inverse
    return (normed, inverse, (normed * gain + shift).astype(jnp.bfloat16))


def norm_back(upstream, normed, inverse, gain):
    scaled = upstream * gain
    first_mean = jnp.mean(scaled, axis=1, keepdims=True)
    second_mean = jnp.mean(scaled * normed, axis=1, keepdims=True)
    through = inverse * (scaled - first_mean - normed * second_mean)
    return (through, jnp.sum(upstream * normed, axis=0), jnp.sum(upstream, axis=0))


def whole_rows(part_rows):
    return lax.all_gather(part_rows, "tensor", axis=0, tiled=True)


def whole_grads(part_rows):
    return lax.all_gather(part_rows, "tensor", axis=0, tiled=True)


def branch_sum(partial_rows):
    return lax.psum_scatter(
        partial_rows.astype(jnp.bfloat16), "tensor", scatter_dimension=0, tiled=True
    ).astype(jnp.float32)


def feature_grad_sum(partial_rows):
    return lax.psum_scatter(
        partial_rows.astype(jnp.bfloat16), "tensor", scatter_dimension=0, tiled=True
    ).astype(jnp.float32)


def inner_rows(left, right):
    return lax.dot_general(
        left, right, (((0,), (0,)), ((), ())), preferred_element_type=jnp.float32
    )


def against_cols(left, right):
    return lax.dot_general(
        left, right, (((1,), (1,)), ((), ())), preferred_element_type=jnp.float32
    )


def distance_onehot(distance_block, table_rows):
    flat_index = distance_block.reshape(1, -1)
    return (
        lax.broadcasted_iota(jnp.int32, (table_rows, flat_index.shape[1]), 0) == flat_index
    ).astype(jnp.bfloat16)


def pair_bias_block(distance_block, table_heads):
    onehot = distance_onehot(distance_block, table_heads.shape[1])
    looked = jnp.dot(table_heads, onehot, preferred_element_type=jnp.float32)
    return looked.astype(jnp.bfloat16).reshape(
        table_heads.shape[0], distance_block.shape[0], distance_block.shape[1]
    )


def split_heads(matrix, block_count, head_count):
    return matrix.reshape(block_count, -1, head_count, matrix.shape[1] // head_count)


def scores_of(query_heads, key_heads, bias, graph_rows, score_scale):
    raw_scores = jnp.einsum(
        "bihd,bjhd->bhij", query_heads, key_heads, preferred_element_type=jnp.float32
    ) * score_scale + bias.astype(jnp.float32)
    same_graph = (graph_rows[:, :, None] == graph_rows[:, None, :])[:, None]
    return jnp.where(same_graph, raw_scores, masked_score)


def attend_forward(inputs, score_scale):
    query, keys, values, bias, graph_rows = inputs
    block_count = graph_rows.shape[0]
    head_count = bias.shape[1]
    query_heads = split_heads(query, block_count, head_count)
    key_heads = split_heads(keys, block_count, head_count)
    value_heads = split_heads(values, block_count, head_count)
    scores = scores_of(query_heads, key_heads, bias, graph_rows, score_scale)
    row_max = jnp.max(scores, axis=-1, keepdims=True)
    shifted = jnp.exp(scores - row_max)
    row_total = jnp.sum(shifted, axis=-1, keepdims=True)
    probs_low = (shifted / row_total).astype(jnp.bfloat16)
    mixed = jnp.einsum(
        "bhij,bjhd->bihd", probs_low, value_heads, preferred_element_type=jnp.float32
    )
    return (mixed.reshape(query.shape).astype(jnp.bfloat16), (row_max + jnp.log(row_total))[..., 0])


def attend_back(inputs, score_scale):
    query, keys, values, mixed_grad, bias, graph_rows, log_total = inputs
    block_count = graph_rows.shape[0]
    head_count = bias.shape[1]
    query_heads = split_heads(query, block_count, head_count)
    key_heads = split_heads(keys, block_count, head_count)
    value_heads = split_heads(values, block_count, head_count)
    grad_heads = split_heads(mixed_grad, block_count, head_count)
    scores = scores_of(query_heads, key_heads, bias, graph_rows, score_scale)
    probs = jnp.exp(scores - log_total[..., None])
    probs_low = probs.astype(jnp.bfloat16)
    values_grad = jnp.einsum(
        "bhij,bihd->bjhd", probs_low, grad_heads, preferred_element_type=jnp.float32
    )
    probs_grad = jnp.einsum(
        "bihd,bjhd->bhij", grad_heads, value_heads, preferred_element_type=jnp.float32
    )
    scores_grad = (
        probs * (probs_grad - jnp.sum(probs * probs_grad, axis=-1, keepdims=True))
    ).astype(jnp.bfloat16)
    query_grad = (
        jnp.einsum("bhij,bjhd->bihd", scores_grad, key_heads, preferred_element_type=jnp.float32)
        * score_scale
    )
    keys_grad = (
        jnp.einsum("bhij,bihd->bjhd", scores_grad, query_heads, preferred_element_type=jnp.float32)
        * score_scale
    )
    stacked = jnp.stack(
        [
            query_grad.reshape(query.shape),
            keys_grad.reshape(query.shape),
            values_grad.reshape(query.shape),
        ],
        axis=1,
    ).astype(jnp.bfloat16)
    return (stacked, scores_grad)


def shards(
    node_features,
    graph_ids,
    degree,
    distance,
    out_grad,
    qkv_weight,
    qv_bias,
    out_weight,
    out_bias,
    norm1_gain,
    norm1_shift,
    ffn_in_weight,
    ffn_in_bias,
    ffn_out_weight,
    ffn_out_bias,
    norm2_gain,
    norm2_shift,
    degree_table,
    spatial_table,
):
    block_count, block_size = graph_ids.shape
    row_count = block_count * block_size
    local_width = qkv_weight.shape[1]
    model_width = qkv_weight.shape[2]
    head_count = spatial_table.shape[0]
    table_rows = spatial_table.shape[1]
    score_scale = 1.0 / math.sqrt(local_width // head_count)
    group_blocks = 4
    group_count = block_count // group_blocks

    def grouped(array):
        return array.reshape((group_count, -1) + array.shape[1:])

    degree_onehot = (
        degree[:, None] == lax.broadcasted_iota(jnp.int32, (1, degree_table.shape[0]), 1)
    ).astype(jnp.bfloat16)
    embedded = node_features.astype(jnp.float32) + jnp.dot(
        degree_onehot, degree_table, preferred_element_type=jnp.float32
    )
    normed1, inverse1, act1 = norm_rows(embedded, norm1_gain, norm1_shift)
    whole1 = whole_rows(act1)
    qkv_flat = qkv_weight.reshape(3 * local_width, model_width)
    projected = against_cols(whole1, qkv_flat).reshape(row_count, 3, local_width)
    query = (projected[:, 0] + qv_bias[0]).astype(jnp.bfloat16)
    keys = projected[:, 1].astype(jnp.bfloat16)
    values = (projected[:, 2] + qv_bias[1]).astype(jnp.bfloat16)
    distance_blocks = distance.reshape(block_count, block_size, block_size)
    pair_bias = lax.map(
        lambda distance_block: pair_bias_block(distance_block, spatial_table), distance_blocks
    )
    mixed_groups, log_totals = lax.map(
        lambda inputs: attend_forward(inputs, score_scale),
        (grouped(query), grouped(keys), grouped(values), grouped(pair_bias), grouped(graph_ids)),
    )
    mixed = mixed_groups.reshape(row_count, local_width)
    attended = branch_sum(jnp.dot(mixed, out_weight, preferred_element_type=jnp.float32)) + out_bias
    residual1 = embedded + attended
    normed2, inverse2, act2 = norm_rows(residual1, norm2_gain, norm2_shift)
    upstream = out_grad.astype(jnp.float32)
    ffn_out_bias_grad = jnp.sum(upstream, axis=0)
    whole2 = whole_rows(act2)
    pre_act = against_cols(whole2, ffn_in_weight) + ffn_in_bias
    hidden = jax.nn.gelu(pre_act, approximate=False).astype(jnp.bfloat16)
    ffn_branch = branch_sum(jnp.dot(hidden, ffn_out_weight, preferred_element_type=jnp.float32))
    layer_out = (residual1 + ffn_branch + ffn_out_bias).astype(jnp.bfloat16)
    grad_whole = whole_grads(out_grad)
    ffn_out_grad = inner_rows(hidden, grad_whole)
    hidden_grad = against_cols(grad_whole, ffn_out_weight)
    unused_value, gelu_pull = jax.vjp(
        lambda pre_value: jax.nn.gelu(pre_value, approximate=False), pre_act
    )
    pre_grad = gelu_pull(hidden_grad)[0].astype(jnp.bfloat16)
    ffn_in_bias_grad = jnp.sum(pre_grad.astype(jnp.float32), axis=0)
    ffn_in_grad = inner_rows(pre_grad, whole2)
    normed2_grad = feature_grad_sum(
        jnp.dot(pre_grad, ffn_in_weight, preferred_element_type=jnp.float32)
    )
    through2, norm2_gain_grad, norm2_shift_grad = norm_back(
        normed2_grad, normed2, inverse2, norm2_gain
    )
    residual1_grad = upstream + through2
    out_bias_grad = jnp.sum(residual1_grad, axis=0)
    attn_whole = whole_grads(residual1_grad.astype(jnp.bfloat16))
    out_weight_grad = inner_rows(mixed, attn_whole)
    mixed_grad = against_cols(attn_whole, out_weight).astype(jnp.bfloat16)
    stacked_groups, scores_grads = lax.map(
        lambda inputs: attend_back(inputs, score_scale),
        (
            grouped(query),
            grouped(keys),
            grouped(values),
            grouped(mixed_grad),
            grouped(pair_bias),
            grouped(graph_ids),
            log_totals,
        ),
    )
    stacked = stacked_groups.reshape(row_count, 3, local_width)
    stacked_float = stacked.astype(jnp.float32)
    qv_bias_grad = jnp.stack(
        [jnp.sum(stacked_float[:, 0], axis=0), jnp.sum(stacked_float[:, 2], axis=0)]
    )
    stacked_flat = stacked.reshape(row_count, 3 * local_width)
    qkv_weight_grad = inner_rows(stacked_flat, whole1).reshape(3, local_width, model_width)
    normed1_grad = feature_grad_sum(
        jnp.dot(stacked_flat, qkv_flat, preferred_element_type=jnp.float32)
    )

    def table_step(running, block_pair):
        distance_block, grad_block = block_pair
        onehot = distance_onehot(distance_block, table_rows)
        return (running + against_cols(grad_block.reshape(head_count, -1), onehot), None)

    spatial_grad, unused_carry = lax.scan(
        table_step,
        jnp.zeros((head_count, table_rows), jnp.float32),
        (distance_blocks, scores_grads.reshape(block_count, head_count, block_size, block_size)),
    )
    through1, norm1_gain_grad, norm1_shift_grad = norm_back(
        normed1_grad, normed1, inverse1, norm1_gain
    )
    embedded_grad = residual1_grad + through1
    input_grad = embedded_grad.astype(jnp.bfloat16)
    grad_upper = embedded_grad.astype(jnp.bfloat16)
    grad_lower = (embedded_grad - grad_upper.astype(jnp.float32)).astype(jnp.bfloat16)
    degree_grad = inner_rows(degree_onehot, grad_upper) + inner_rows(degree_onehot, grad_lower)
    (
        ffn_in_grad,
        ffn_in_bias_grad,
        ffn_out_grad,
        qkv_weight_grad,
        qv_bias_grad,
        out_weight_grad,
        spatial_grad,
    ) = lax.psum(
        (
            ffn_in_grad,
            ffn_in_bias_grad,
            ffn_out_grad,
            qkv_weight_grad,
            qv_bias_grad,
            out_weight_grad,
            spatial_grad,
        ),
        "dp",
    )
    (
        degree_grad,
        out_bias_grad,
        ffn_out_bias_grad,
        norm1_gain_grad,
        norm1_shift_grad,
        norm2_gain_grad,
        norm2_shift_grad,
    ) = lax.psum(
        (
            degree_grad,
            out_bias_grad,
            ffn_out_bias_grad,
            norm1_gain_grad,
            norm1_shift_grad,
            norm2_gain_grad,
            norm2_shift_grad,
        ),
        ("dp", "tensor"),
    )
    return (
        layer_out,
        input_grad,
        qkv_weight_grad,
        qv_bias_grad,
        out_weight_grad,
        out_bias_grad,
        norm1_gain_grad,
        norm1_shift_grad,
        ffn_in_grad,
        ffn_in_bias_grad,
        ffn_out_grad,
        ffn_out_bias_grad,
        norm2_gain_grad,
        norm2_shift_grad,
        degree_grad,
        spatial_grad,
    )


def solution(mesh):
    return jax.shard_map(
        shards,
        mesh=mesh,
        in_specs=(
            P(("dp", "tensor"), None),
            P("dp", None),
            P(("dp", "tensor")),
            P("dp", None),
            P(("dp", "tensor"), None),
            P(None, "tensor", None),
            P(None, "tensor"),
            P("tensor", None),
            P(),
            P(),
            P(),
            P("tensor", None),
            P("tensor"),
            P("tensor", None),
            P(),
            P(),
            P(),
            P(),
            P("tensor", None),
        ),
        out_specs=(
            P(("dp", "tensor"), None),
            P(("dp", "tensor"), None),
            P(None, "tensor", None),
            P(None, "tensor"),
            P("tensor", None),
            P(),
            P(),
            P(),
            P("tensor", None),
            P("tensor"),
            P("tensor", None),
            P(),
            P(),
            P(),
            P(),
            P("tensor", None),
        ),
        check_vma=False,
    )
```

profile of v0, /device:TPU:0, one launch (start us, length us, event | category | flops | bytes accessed | tf_op | source)
XLA Modules:
  0.0 616.1 jit_solution(1584065396677808624)
XLA Ops:
  10.4 54.4 %while.45 = (s32[]{:T(128)}, bf16[8,8,128,128]{2,3,1,0:T(8,128)(2,1)}, s32[8,128,128]{2,1,0:T(8,128)}, bf16[8,512]{1,0:T(8,128)(2,1)S(1)}, s32[]{:T(128)}) while((s32[]{:T(128)}, bf16[8,8,128,128]{2,3,1,0:T(8,128)(2,1)}, s32[8,128,128]{2,1,0:T(8,128)}, bf16[8,512]{1,0:T(8,128)(2,1)S(1)}, s32[]{:T(128)}) %tuple.145), condition=%wide.region_3.4_spmd, body=%wide.region_2.3_spmd.sunk | while | flops 142737408 | bytes 1515597 | solution.py:192
  11.3 5.0 fusion.125
  18.1 5.0 fusion.125
  24.9 5.0 fusion.125
  31.7 5.0 fusion.125
  38.5 5.0 fusion.125
  45.3 5.0 fusion.125
  52.1 5.0 fusion.125
  58.8 5.0 fusion.125
  64.8 2.5 fusion.35
  71.2 2.7 squeeze.31
  74.0 2.3 fusion.53
  76.3 10.7 %while.46 = (s32[]{:T(128)}, bf16[2,512,192]{1,2,0:T(8,128)(2,1)S(1)}, f32[2,4,8,128]{3,2,1,0:T(8,128)S(1)}, bf16[2,512,192]{1,2,0:T(8,128)(2,1)}, s32[2,4,128]{...) while((s32[]{:T(128)}, ...), condition=%wide.region_7.8_spmd, body=%wide.region_4.7_spmd.sunk | while | flops 55734272 | bytes 11933821 | solution.py:195
  83.8 1.9 fusion.127
  87.0 2.9 convolution_convert_fusion.5
  90.0 38.2 %reduce-scatter.5.cloned.1.call-done = bf16[256,768]{1,0:T(8,128)(2,1)} async-done(((bf16[1024,768]{1,0:T(8,128)(2,1)}), bf16[256,768]{1,0:T(8,128)(2,1)}) %reduce-scatter.5.cloned.1.call-update) | async-done | bytes 393232 | tf_op jit(solution)/shard_map/reduce_scatter | solution.py:37
  131.2 10.5 %reduce-scatter.9.cloned.1.call-start = ((), (), s32[]{:S(2)}) async-start(), calls=%async_computation.9 | async-start | bytes 1966080 | tf_op jit(solution)/shard_map/reduce_scatter | solution.py:43
  141.7 25.0 %all-gather.7.cloned.1.call-done = bf16[1024,768]{1,0:T(8,128)(2,1)} async-done(((bf16[256,768]{1,0:T(8,128)(2,1)}), bf16[1024,768]{1,0:T(8,128)(2,1)}) %all-gather.7.cloned.1.call-update) | async-done | bytes 1572880 | tf_op jit(solution)/shard_map/all_gather | solution.py:29
  166.7 2.1 convolution_add_fusion.1
  168.8 35.3 %all-gather.9.cloned.1.call-done = bf16[1024,768]{1,0:T(8,128)(2,1)} async-done(((bf16[256,768]{1,0:T(8,128)(2,1)}), bf16[1024,768]{1,0:T(8,128)(2,1)}) %all-gather.9.cloned.1.call-update) | async-done | bytes 1572880 | tf_op jit(solution)/shard_map/all_gather | solution.py:33
  204.0 4.6 convert_reduce_fusion.3
  211.8 2.9 convolution_convert_fusion.4
  214.7 30.2 %reduce-scatter.9.cloned.1.call-done = bf16[256,768]{1,0:T(8,128)(2,1)} async-done(((bf16[1024,768]{1,0:T(8,128)(2,1)}), bf16[256,768]{1,0:T(8,128)(2,1)}) %reduce-scatter.9.cloned.1.call-update) | async-done | bytes 393232 | tf_op jit(solution)/shard_map/reduce_scatter | solution.py:43
  246.4 35.6 %reduce-scatter.7.cloned.1.call-done = bf16[256,768]{1,0:T(8,128)(2,1)} async-done(((bf16[1024,768]{1,0:T(8,128)(2,1)}), bf16[256,768]{1,0:T(8,128)(2,1)}) %reduce-scatter.7.cloned.1.call-update) | async-done | bytes 393232 | tf_op jit(solution)/shard_map/reduce_scatter | solution.py:37
  282.0 2.4 fusion.64
  285.3 35.9 %all-gather.11.cloned.1.call-done = bf16[1024,768]{1,0:T(8,128)(2,1)} async-done(((bf16[256,768]{1,0:T(8,128)(2,1)}), bf16[1024,768]{1,0:T(8,128)(2,1)}) %all-gather.11.cloned.1.call-update) | async-done | bytes 1572880 | tf_op jit(solution)/shard_map/all_gather | solution.py:33
  321.3 2.1 convolution_convert_fusion.6
  324.1 21.3 %while.47 = (s32[]{:T(128)}, bf16[2,512,3,192]{1,3,2,0:T(8,128)(2,1)}, bf16[2,4,8,128,128]{4,3,2,1,0:T(8,128)(2,1)}, bf16[2,512,192]{1,2,0:T(8,128)(2,1)S(1)}, s...) while((s32[]{:T(128)}, ...), condition=%wide.region_17.18_spmd, body=%wide.region_15.17_spmd.sunk | while | flops 133918720 | bytes 29841552 | solution.py:230
  327.0 2.2 multiply_reduce_fusion.4
  337.6 2.2 multiply_reduce_fusion.4
  345.4 2.5 copy.98
  349.2 2.6 convolution_convert_fusion.2
  353.2 2.4 fusion.74
  358.2 2.3 fusion.33
  360.8 25.4 %reduce-scatter.11.cloned.1.call-done = bf16[256,768]{1,0:T(8,128)(2,1)} async-done(((bf16[1024,768]{1,0:T(8,128)(2,1)}), bf16[256,768]{1,0:T(8,128)(2,1)}) %reduce-scatter.11.cloned.1.call-update) | async-done | bytes 393232 | tf_op jit(solution)/shard_map/reduce_scatter | solution.py:43
  391.3 58.4 %while.48 = (s32[]{:T(128)}, f32[8,512]{1,0:T(8,128)S(1)}, bf16[8,8,128,128]{3,2,1,0:T(8,128)(2,1)}, s32[8,128,128]{2,1,0:T(8,128)}, s32[]{:T(128)}, /*index=5*/s32[]{:T(128)}) while((s32[]{:T(128)}, f32[8,512]{1,0:T(8,128)S(1)}, bf16[8,8,128,128]{3,2,1,0:T(8,128)(2,1)}, s32[8,128,128]{2,1,0:T(8,128)}, s32[]{:T(128)}, ...), condition=%wide.region_44.45_spmd.clone, body=%wide.region_43.44_spmd.clone.sunk | while | flops 142614528 | bytes 1015903 | solution.py:258
  393.3 5.5 fusion.144
  400.5 5.5 fusion.144
  407.8 5.5 fusion.144
  415.1 5.5 fusion.144
  422.4 5.5 fusion.144
  429.7 5.5 fusion.144
  437.0 5.5 fusion.144
  444.3 5.5 fusion.144
  450.6 24.9 %all-reduce.1 = (f32[2,192]{1,0:T(2,128)}, f32[192]{0:T(256)}, f32[8,512]{1,0:T(8,128)}) all-reduce(f32[2,192]{1,0:T(2,128)S(1)} %pad_maximum_fusion, f32[192]{0:T(256)S(1)} %get-tuple-element.308, f32[8,512]{1,0:T(8,128)S(1)} %get-tuple-element.161), channel_id=1, replica_groups=mesh['dp'=8,'tensor'=4] {'dp'}, use_global_device_ids=true, to_apply=%region_24.25 | all-reduce | flops 4672 | bytes 37376 | tf_op jit(solution)/shard_map/psum | solution.py:279
  475.5 39.5 %all-reduce = (f32[768]{0:T(1024)}, f32[768]{0:T(1024)}, f32[768]{0:T(1024)}, f32[768]{0:T(1024)}, f32[768]{0:T(1024)}, /*index=5*/f32[768]{0:T(1024)}) all-reduce(f32[768]{0:T(1024)S(1)} %get-tuple-element.306, f32[768]{0:T(1024)S(1)} %get-tuple-element.235, ...), channel_id=1, replica_groups=mesh['dp'=8,'tensor'=4] {'dp','tensor'}, use_global_device_ids=true, to_apply=%region_27.28 | all-reduce | flops 4608 | bytes 36864 | tf_op jit(solution)/shard_map/psum | solution.py:299
  515.0 87.4 %all-reduce.6.cloned.1.call-done = f32[512,768]{1,0:T(8,128)} async-done(((f32[512,768]{1,0:T(8,128)}), f32[512,768]{1,0:T(8,128)}) %all-reduce.6.cloned.1.call-update) | async-done | bytes 1572880 | tf_op jit(solution)/shard_map/psum | solution.py:299
  602.4 2.9 copy.228
  (255 shorter events, 85.5 us)
Async XLA Ops:
  7.2 57.7 %copy-start = (bf16[3,192,768]{2,1,0:T(8,128)(2,1)S(1)}, bf16[3,192,768]{2,1,0:T(8,128)(2,1)}, u32[]{:S(2)}) copy-start(bf16[3,192,768]{2,1,0:T(8,128)(2,1)} %param.32) | copy-start | bytes 2654212
  7.2 2.1 copy-start.27
  7.2 2.1 copy-start.29
  7.2 3.2 copy-start.36
  7.2 57.6 %all-gather.5.cloned.1.call-start = ((), (), s32[]{:S(2)}) async-start(), calls=%async_computation.4 | async-start | bytes 1966080 | tf_op jit(solution)/shard_map/all_gather | solution.py:29
  9.1 119.2 %copy-start.1 = (f32[256,768]{1,0:T(8,128)}, f32[256,768]{1,0:T(8,128)S(1)}, u32[]{:S(2)}) copy-start(f32[256,768]{1,0:T(8,128)S(1)} %get-tuple-element.332) | copy-start | bytes 2359300
  10.3 117.9 %reduce-scatter.5.cloned.1.call-start = ((), (), s32[]{:S(2)}) async-start(), calls=%async_computation.5 | async-start | bytes 1966080 | tf_op jit(solution)/shard_map/reduce_scatter | solution.py:37
  10.4 54.4 %copy-start.33 = (f32[2,192]{1,0:T(2,128)S(1)}, f32[2,192]{1,0:T(2,128)}, u32[]{:S(2)}) copy-start(f32[2,192]{1,0:T(2,128)} %param.33) | copy-start | bytes 4612
  71.2 5.1 copy-start.23
  71.2 5.1 copy-start.25
  87.0 3.0 copy-start.8
  87.0 41.3 %copy-start.30 = (f32[768]{0:T(1024)S(1)}, f32[768]{0:T(1024)}, u32[]{:S(2)}) copy-start(f32[768]{0:T(1024)} %param.35) | copy-start | bytes 9220
  89.9 39.8 %copy-start.26 = (f32[768]{0:T(1024)S(1)}, f32[768]{0:T(1024)}, u32[]{:S(2)}) copy-start(f32[768]{0:T(1024)} %param.42) | copy-start | bytes 9220
  89.9 39.8 %copy-start.31 = (f32[768]{0:T(1024)S(1)}, f32[768]{0:T(1024)}, u32[]{:S(2)}) copy-start(f32[768]{0:T(1024)} %param.43) | copy-start | bytes 9220
  89.9 76.8 %copy-start.16 = (bf16[192,768]{1,0:T(8,128)(2,1)S(1)}, bf16[192,768]{1,0:T(8,128)(2,1)}, u32[]{:S(2)}) copy-start(bf16[192,768]{1,0:T(8,128)(2,1)} %param.38) | copy-start | bytes 884740
  89.9 76.8 %copy-start.34 = (f32[192]{0:T(256)S(1)}, f32[192]{0:T(256)}, u32[]{:S(2)}) copy-start(f32[192]{0:T(256)} %param.39) | copy-start | bytes 2308
  89.9 76.8 %all-gather.7.cloned.1.call-start = ((), (), s32[]{:S(2)}) async-start(), calls=%async_computation.6 | async-start | bytes 1966080 | tf_op jit(solution)/shard_map/all_gather | solution.py:29
  130.7 73.4 %all-gather.9.cloned.1.call-start = ((), (), s32[]{:S(2)}) async-start(), calls=%async_computation.8 | async-start | bytes 1966080 | tf_op jit(solution)/shard_map/all_gather | solution.py:33
  131.2 113.7 %reduce-scatter.9.cloned.1.call-start = ((), (), s32[]{:S(2)}) async-start(), calls=%async_computation.9 | async-start | bytes 1966080 | tf_op jit(solution)/shard_map/reduce_scatter | solution.py:43
  204.0 4.6 copy-start.17
  208.7 1.9 copy-start.15
  210.4 71.5 %reduce-scatter.7.cloned.1.call-start = ((), (), s32[]{:S(2)}) async-start(), calls=%async_computation.7 | async-start | bytes 1966080 | tf_op jit(solution)/shard_map/reduce_scatter | solution.py:37
  211.8 34.6 %copy-start.10 = (bf16[1024,192]{0,1:T(8,128)(2,1)}, bf16[1024,192]{0,1:T(8,128)(2,1)S(1)}, u32[]{:S(2)}) copy-start(bf16[1024,192]{0,1:T(8,128)(2,1)S(1)} %multiply_convert_fusion.1) | copy-start | bytes 1179652
  211.8 70.2 %copy-start.32 = (f32[768]{0:T(1024)S(1)}, f32[768]{0:T(1024)}, u32[]{:S(2)}) copy-start(f32[768]{0:T(1024)} %param.41) | copy-start | bytes 9220
  214.7 106.6 %all-gather.11.cloned.1.call-start = ((), (), s32[]{:S(2)}) async-start(), calls=%async_computation.10 | async-start | bytes 1966080 | tf_op jit(solution)/shard_map/all_gather | solution.py:33
  246.4 74.9 %copy-start.24 = (bf16[192,768]{1,0:T(8,128)(2,1)S(1)}, bf16[192,768]{1,0:T(8,128)(2,1)}, u32[]{:S(2)}) copy-start(bf16[192,768]{1,0:T(8,128)(2,1)} %param.34) | copy-start | bytes 884740
  284.4 39.7 %copy-start.3 = (f32[256,768]{1,0:T(8,128)}, f32[256,768]{1,0:T(8,128)S(1)}, u32[]{:S(2)}) copy-start(f32[256,768]{1,0:T(8,128)S(1)} %get-tuple-element.307) | copy-start | bytes 2359300
  285.2 101.0 %reduce-scatter.11.cloned.1.call-start = ((), (), s32[]{:S(2)}) async-start(), calls=%async_computation.11 | async-start | bytes 1966080 | tf_op jit(solution)/shard_map/reduce_scatter | solution.py:43
  348.2 1.0 copy-start.18
  351.8 1.4 copy-start.5
  351.8 3.9 copy-start.11
  351.8 5.1 copy-start.9
  351.8 163.2 %all-reduce.8.cloned.1.call-start = ((), (), s32[]{:S(2)}) async-start(), calls=%async_computation.13 | async-start | bytes 7077888 | tf_op jit(solution)/shard_map/psum | solution.py:279
  353.2 2.4 copy-start.12
  353.2 3.8 copy-start.13
  355.6 2.6 copy-start.19
  355.6 2.6 copy-start.35
  360.5 25.7 %copy-start.2 = (f32[256,768]{1,0:T(8,128)S(1)}, f32[256,768]{1,0:T(8,128)}, u32[]{:S(2)}) copy-start(f32[256,768]{1,0:T(8,128)} %copy-done.1) | copy-start | bytes 2359300
  360.5 27.1 %copy-start.4 = (f32[256,768]{1,0:T(8,128)S(1)}, f32[256,768]{1,0:T(8,128)}, u32[]{:S(2)}) copy-start(f32[256,768]{1,0:T(8,128)} %copy-done.3) | copy-start | bytes 2359300
  360.6 241.8 %all-reduce.6.cloned.1.call-start = ((), (), s32[]{:S(2)}) async-start(), calls=%async_computation.12 | async-start | bytes 3145728 | tf_op jit(solution)/shard_map/psum | solution.py:299
  360.8 28.2 %copy-start.28 = (s32[256]{0:T(256)S(1)}, s32[256]{0:T(256)}, u32[]{:S(2)}) copy-start(s32[256]{0:T(256)} %param.29) | copy-start | bytes 3076
  389.0 2.3 copy-start.7
  391.3 58.4 %copy-start.6 = (bf16[2,512,3,192]{1,3,2,0:T(8,128)(2,1)S(1)}, bf16[2,512,3,192]{1,3,2,0:T(8,128)(2,1)}, u32[]{:S(2)}) copy-start(bf16[2,512,3,192]{1,3,2,0:T(8,128)(2,1)} %get-tuple-element.159) | copy-start | bytes 3538948
  515.0 90.3 %copy-start.22 = (f32[192,768]{1,0:T(8,128)S(1)}, f32[192,768]{1,0:T(8,128)}, u32[]{:S(2)}) copy-start(f32[192,768]{1,0:T(8,128)} %get-tuple-element.612) | copy-start | bytes 1769476
  602.4 3.7 copy-start.21
  602.4 4.5 copy-start.20
  605.3 2.5 copy-start.14
Sparse Core Ops, SparseCore 0:
  10.4 39.8 all-gather.4
  90.0 38.1 reduce-scatter.4
  130.8 35.8 all-gather.6
  168.1 35.8 all-gather.8
  210.6 34.2 reduce-scatter.8
  247.6 34.2 reduce-scatter.6
  285.4 35.8 all-gather.10
  351.9 34.2 reduce-scatter.10
  391.0 72.7 all-reduce.7
  469.6 132.7 all-reduce.5
where the time goes:
time: 627 us; the launch traced here: 616 us
  waiting for transfers between devices  314 us (50%)
  matrix products  130 us (21%)
  blocking collectives  64.4 us (10%)
  local copies, waits for them, and re-layouts  62.3 us (10%)
  other arithmetic  19 us (3%)
  between operations  15 us (2%)
  starting transfers between devices  11 us (2%)
    psum x1, waiting for transfers between devices, shards(): lax.psum((degree_grad, out_bias_grad, ffn_out_bias_grad, norm1_gain_grad,...  87.4 us
    reduce_scatter x2, waiting for transfers between devices, branch_sum(): lax.psum_scatter(partial_rows.astype(jnp.bfloat16), 'tensor', scatter_dim...  73.8 us
    all_gather x2, waiting for transfers between devices, whole_grads(): return lax.all_gather(part_rows, 'tensor', axis=0, tiled=True)  71.2 us
    reduce_scatter x2, waiting for transfers between devices, feature_grad_sum(): lax.psum_scatter(partial_rows.astype(jnp.bfloat16), 'tensor', scatter_dim...  55.6 us
    dot_general x12, matrix products, against_cols(): lax.dot_general(left, right, (((1,), (1,)), ((), ())), preferred_element_...  55.1 us
    dot_general x8, matrix products, pair_bias_block(): looked = jnp.dot(table_heads, onehot, preferred_element_type=jnp.float32)  40 us
    psum x1, blocking collectives, shards(): lax.psum((degree_grad, out_bias_grad, ffn_out_bias_grad, norm1_gain_grad,...  39.5 us
    all_gather x2, waiting for transfers between devices, whole_rows(): return lax.all_gather(part_rows, 'tensor', axis=0, tiled=True)  25 us
  transfers between devices with their start and end apart: 10, of which 8 were waited for; matrix products, arithmetic and copies ran while one was open for 22% of the time, Pallas kernels for 0%

commit v1 on v0

--- a/solution.py
+++ b/solution.py
@@ -6,6 +6,22 @@
 
 norm_eps = 1e-05
 masked_score = -1e30
+
+
+def ring_gather(x, axis, dim):
+    ways, here, turn = (lax.axis_size(axis), lax.axis_index(axis), x.shape[dim])
+    shape = [n * ways if d == dim else n for d, n in enumerate(x.shape)]
+    full = lax.dynamic_update_slice_in_dim(jnp.zeros(shape, x.dtype), x, here * turn, axis=dim)
+    going_up = going_down = x
+    for far in range(1, ways // 2 + 1):
+        going_up = lax.ppermute(going_up, axis, [(d, (d + 1) % ways) for d in range(ways)])
+        full = lax.dynamic_update_slice_in_dim(full, going_up, (here - far) % ways * turn, axis=dim)
+        if 2 * far < ways:
+            going_down = lax.ppermute(going_down, axis, [(d, (d - 1) % ways) for d in range(ways)])
+            full = lax.dynamic_update_slice_in_dim(
+                full, going_down, (here + far) % ways * turn, axis=dim
+            )
+    return full
 
 
 def norm_rows(hidden_rows, gain, shift):
@@ -30,7 +46,7 @@
 
 
 def whole_grads(part_rows):
-    return lax.all_gather(part_rows, "tensor", axis=0, tiled=True)
+    return ring_gather(part_rows, "tensor", 0)
 
 
 def branch_sum(partial_rows):

time: 627 us -> 604 us (0.963)
  waiting for transfers between devices: 314 us -> 265 us
  starting transfers between devices: 11 us -> 26.7 us
  local copies, waits for them, and re-layouts: 62.3 us -> 70 us
    all_gather x2 -> x0, waiting for transfers between devices: 71.2 us -> none  [whole_grads(): return lax.all_gather(part_rows, 'tensor', axis=0, tiled=True)]
    ppermute x0 -> x6, waiting for transfers between devices: none -> 46.7 us  [the longest x4 40.5 us: ring_gather(): lax.ppermute(going_up, axis, [(d, (d + 1) % ways) for d in range(ways)])]
    ppermute x0 -> x6, starting transfers between devices: none -> 26.2 us  [the longest x4 18.8 us: ring_gather(): lax.ppermute(going_up, axis, [(d, (d + 1) % ways) for d in range(ways)])]
    all_gather x2, waiting for transfers between devices: 25 us -> 3.68 us  [whole_rows(): return lax.all_gather(part_rows, 'tensor', axis=0, tiled=True)]
    reduce_scatter x2, starting transfers between devices: 10.5 us -> 0.08 us  [feature_grad_sum(): lax.psum_scatter(partial_rows.astype(jnp.bfloat16), 'tensor', scatter_dim...]
    dynamic_update_slice x0 -> x7, local copies, waits for them, and re-layouts: none -> 6.39 us  [the longest x4 4.08 us: ring_gather(): lax.dynamic_update_slice_in_dim(full, going_up, (here - far) % ways * tur...]
  transfers between devices with their start and end apart: 10 -> 14, of which waited for: 8 -> 12; matrix products, arithmetic and copies ran while one was open for 22% -> 24% of each run, Pallas kernels for 0% -> 0%
where the time goes in v1:
time: 604 us; the launch traced here: 593 us
  waiting for transfers between devices  265 us (44%)
  matrix products  132 us (22%)
  local copies, waits for them, and re-layouts  70 us (12%)
  blocking collectives  64.4 us (11%)
  starting transfers between devices  26.7 us (4%)
  other arithmetic  19 us (3%)
  between operations  15 us (2%)
    psum x1, waiting for transfers between devices, shards(): lax.psum((degree_grad, out_bias_grad, ffn_out_bias_grad, norm1_gain_grad,...  87.6 us
    reduce_scatter x2, waiting for transfers between devices, branch_sum(): lax.psum_scatter(partial_rows.astype(jnp.bfloat16), 'tensor', scatter_dim...  73.3 us
    dot_general x12, matrix products, against_cols(): lax.dot_general(left, right, (((1,), (1,)), ((), ())), preferred_element_...  55.1 us
    reduce_scatter x2, waiting for transfers between devices, feature_grad_sum(): lax.psum_scatter(partial_rows.astype(jnp.bfloat16), 'tensor', scatter_dim...  54 us
    ppermute x4, waiting for transfers between devices, ring_gather(): lax.ppermute(going_up, axis, [(d, (d + 1) % ways) for d in range(ways)])  40.5 us
    dot_general x8, matrix products, pair_bias_block(): looked = jnp.dot(table_heads, onehot, preferred_element_type=jnp.float32)  40 us
    psum x1, blocking collectives, shards(): lax.psum((degree_grad, out_bias_grad, ffn_out_bias_grad, norm1_gain_grad,...  39.5 us
    psum x1, blocking collectives, shards(): lax.psum((ffn_in_grad, ffn_in_bias_grad, ffn_out_grad, qkv_weight_grad, q...  24.9 us
  transfers between devices with their start and end apart: 14, of which 12 were waited for; matrix products, arithmetic and copies ran while one was open for 24% of the time, Pallas kernels for 0%

profile of v1, /device:TPU:0, one launch (start us, length us, event | category | flops | bytes accessed | tf_op | source)
XLA Modules:
  0.0 593.0 jit_solution(8676907522961289133)
XLA Ops:
  10.4 54.4 %while.45 = (s32[]{:T(128)}, bf16[8,8,128,128]{2,3,1,0:T(8,128)(2,1)}, s32[8,128,128]{2,1,0:T(8,128)}, bf16[8,512]{1,0:T(8,128)(2,1)S(1)}, s32[]{:T(128)}) while((s32[]{:T(128)}, bf16[8,8,128,128]{2,3,1,0:T(8,128)(2,1)}, s32[8,128,128]{2,1,0:T(8,128)}, bf16[8,512]{1,0:T(8,128)(2,1)S(1)}, s32[]{:T(128)}) %tuple.143), condition=%wide.region_3.4_spmd, body=%wide.region_2.3_spmd.sunk | while | flops 142737408 | bytes 1515597 | solution.py:208
  11.3 5.0 fusion.125
  18.1 5.0 fusion.125
  24.9 5.0 fusion.125
  31.7 5.0 fusion.125
  38.5 5.0 fusion.125
  45.3 5.0 fusion.125
  52.1 5.0 fusion.125
  58.9 5.0 fusion.125
  64.9 2.5 fusion.35
  71.2 2.7 squeeze.31
  76.3 10.6 %while.46 = (s32[]{:T(128)}, bf16[2,512,192]{1,2,0:T(8,128)(2,1)S(1)}, f32[2,4,8,128]{3,2,1,0:T(8,128)S(1)}, bf16[2,512,192]{1,2,0:T(8,128)(2,1)}, s32[2,4,128]{...) while((s32[]{:T(128)}, ...), condition=%wide.region_7.8_spmd, body=%wide.region_4.7_spmd.sunk | while | flops 55734272 | bytes 11933821 | solution.py:211
  87.0 2.9 convolution_convert_fusion.5
  90.0 38.2 %reduce-scatter.5.cloned.1.call-done = bf16[256,768]{1,0:T(8,128)(2,1)} async-done(((bf16[1024,768]{1,0:T(8,128)(2,1)}), bf16[256,768]{1,0:T(8,128)(2,1)}) %reduce-scatter.5.cloned.1.call-update) | async-done | bytes 393232 | tf_op jit(solution)/shard_map/reduce_scatter | solution.py:53
  130.9 3.7 collective-permute-start.1
  134.6 12.7 %collective-permute-done = bf16[256,768]{1,0:T(8,128)(2,1)S(1)} collective-permute-done((bf16[256,768]{1,0:T(8,128)(2,1)S(1)}, bf16[256,768]{1,0:T(8,128)(2,1)S(1)}, u32[]{:S(2)}, u32[]{:S(2)}) %collective-permute-start) | collective-permute-done | bytes 393248 | tf_op jit(solution)/shard_map/ppermute | solution.py:17
  147.3 14.7 %collective-permute-start.2 = (bf16[256,768]{1,0:T(8,128)(2,1)S(1)}, bf16[256,768]{1,0:T(8,128)(2,1)}, u32[]{:S(2)}, u32[]{:S(2)}) collective-permute-start(bf16[256,768]{1,0:T(8,128)(2,1)S(1)} %collective-permute-done), channel_id=1, source_target_pairs={{0,1},{1,2},{2,3},{3,0},{4,5},{5,6},{6,7},{7,4},{8,9},{9,10},{10,1... | collective-permute-start | bytes 1179656 | tf_op jit(solution)/shard_map/ppermute | solution.py:17
  164.7 5.6 collective-permute-done.1
  171.1 8.5 %collective-permute-done.2 = bf16[256,768]{1,0:T(8,128)(2,1)} collective-permute-done((bf16[256,768]{1,0:T(8,128)(2,1)S(1)}, bf16[256,768]{1,0:T(8,128)(2,1)}, u32[]{:S(2)}, u32[]{:S(2)}) %collective-permute-start.2) | collective-permute-done | bytes 393248 | tf_op jit(solution)/shard_map/ppermute | solution.py:17
  181.4 3.7 all-gather.5.cloned.1.call-done
  187.1 4.6 convert_reduce_fusion.3
  194.9 2.9 convolution_convert_fusion.4
  197.9 30.6 %reduce-scatter.9.cloned.1.call-done = bf16[256,768]{1,0:T(8,128)(2,1)} async-done(((bf16[1024,768]{1,0:T(8,128)(2,1)}), bf16[256,768]{1,0:T(8,128)(2,1)}) %reduce-scatter.9.cloned.1.call-update) | async-done | bytes 393232 | tf_op jit(solution)/shard_map/reduce_scatter | solution.py:59
  230.0 35.0 %reduce-scatter.7.cloned.1.call-done = bf16[256,768]{1,0:T(8,128)(2,1)} async-done(((bf16[1024,768]{1,0:T(8,128)(2,1)}), bf16[256,768]{1,0:T(8,128)(2,1)}) %reduce-scatter.7.cloned.1.call-update) | async-done | bytes 393232 | tf_op jit(solution)/shard_map/reduce_scatter | solution.py:53
  265.0 2.4 fusion.64
  269.7 3.7 collective-permute-start.4
  273.4 10.0 %collective-permute-done.3 = bf16[256,768]{1,0:T(8,128)(2,1)S(1)} collective-permute-done((bf16[256,768]{1,0:T(8,128)(2,1)S(1)}, bf16[256,768]{1,0:T(8,128)(2,1)S(1)}, u32[]{:S(2)}, u32[]{:S(2)}) %collective-permute-start.3) | collective-permute-done | bytes 393248 | tf_op jit(solution)/shard_map/ppermute | solution.py:17
  283.4 3.8 collective-permute-start.5
  289.4 9.3 %collective-permute-done.5 = bf16[256,768]{1,0:T(8,128)(2,1)S(1)} collective-permute-done((bf16[256,768]{1,0:T(8,128)(2,1)S(1)}, bf16[256,768]{1,0:T(8,128)(2,1)S(1)}, u32[]{:S(2)}, u32[]{:S(2)}) %collective-permute-start.5) | collective-permute-done | bytes 393248 | tf_op jit(solution)/shard_map/ppermute | solution.py:17
  301.6 21.2 %while.47 = (s32[]{:T(128)}, bf16[2,512,3,192]{1,3,2,0:T(8,128)(2,1)}, bf16[2,4,8,128,128]{4,3,2,1,0:T(8,128)(2,1)}, bf16[2,512,192]{1,2,0:T(8,128)(2,1)S(1)}, s...) while((s32[]{:T(128)}, ...), condition=%wide.region_17.18_spmd, body=%wide.region_15.17_spmd.sunk | while | flops 133918720 | bytes 32987336 | solution.py:246
  322.8 2.5 copy.98
  326.6 2.6 convolution_convert_fusion.2
  330.2 2.7 fusion.75
  334.2 2.8 fusion.73
  339.6 23.4 %reduce-scatter.11.cloned.1.call-done = bf16[256,768]{1,0:T(8,128)(2,1)} async-done(((bf16[1024,768]{1,0:T(8,128)(2,1)}), bf16[256,768]{1,0:T(8,128)(2,1)}) %reduce-scatter.11.cloned.1.call-update) | async-done | bytes 393232 | tf_op jit(solution)/shard_map/reduce_scatter | solution.py:59
  368.1 58.4 %while.48 = (s32[]{:T(128)}, f32[8,512]{1,0:T(8,128)S(1)}, bf16[8,8,128,128]{3,2,1,0:T(8,128)(2,1)}, s32[8,128,128]{2,1,0:T(8,128)}, s32[]{:T(128)}, /*index=5*/s32[]{:T(128)}) while((s32[]{:T(128)}, f32[8,512]{1,0:T(8,128)S(1)}, bf16[8,8,128,128]{3,2,1,0:T(8,128)(2,1)}, s32[8,128,128]{2,1,0:T(8,128)}, s32[]{:T(128)}, ...), condition=%wide.region_44.45_spmd.clone, body=%wide.region_43.44_spmd.clone.sunk | while | flops 142614528 | bytes 1015903 | solution.py:274
  370.0 5.5 fusion.144
  377.3 5.5 fusion.144
  384.6 5.5 fusion.144
  391.9 5.5 fusion.144
  399.2 5.5 fusion.144
  406.4 5.5 fusion.144
  413.7 5.5 fusion.144
  421.0 5.5 fusion.144
  427.3 24.9 %all-reduce.1 = (f32[2,192]{1,0:T(2,128)}, f32[192]{0:T(256)}, f32[8,512]{1,0:T(8,128)}) all-reduce(f32[2,192]{1,0:T(2,128)S(1)} %pad_maximum_fusion, f32[192]{0:T(256)S(1)} %get-tuple-element.308, f32[8,512]{1,0:T(8,128)S(1)} %get-tuple-element.161), channel_id=1, replica_groups=mesh['dp'=8,'tensor'=4] {'dp'}, use_global_device_ids=true, to_apply=%region_24.25 | all-reduce | flops 4672 | bytes 37376 | tf_op jit(solution)/shard_map/psum | solution.py:295
  452.2 39.5 %all-reduce = (f32[768]{0:T(1024)}, f32[768]{0:T(1024)}, f32[768]{0:T(1024)}, f32[768]{0:T(1024)}, f32[768]{0:T(1024)}, /*index=5*/f32[768]{0:T(1024)}) all-reduce(f32[768]{0:T(1024)S(1)} %get-tuple-element.306, f32[768]{0:T(1024)S(1)} %get-tuple-element.235, ...), channel_id=1, replica_groups=mesh['dp'=8,'tensor'=4] {'dp','tensor'}, use_global_device_ids=true, to_apply=%region_27.28 | all-reduce | flops 4608 | bytes 36864 | tf_op jit(solution)/shard_map/psum | solution.py:315
  491.7 87.6 %all-reduce.6.cloned.1.call-done = f32[512,768]{1,0:T(8,128)} async-done(((f32[512,768]{1,0:T(8,128)}), f32[512,768]{1,0:T(8,128)}) %all-reduce.6.cloned.1.call-update) | async-done | bytes 1572880 | tf_op jit(solution)/shard_map/psum | solution.py:315
  579.3 2.9 copy.236
  (276 shorter events, 107.3 us)
Async XLA Ops:
  7.2 57.7 %copy-start = (bf16[3,192,768]{2,1,0:T(8,128)(2,1)S(1)}, bf16[3,192,768]{2,1,0:T(8,128)(2,1)}, u32[]{:S(2)}) copy-start(bf16[3,192,768]{2,1,0:T(8,128)(2,1)} %param.32) | copy-start | bytes 2654212
  7.2 2.1 copy-start.28
  7.2 2.1 copy-start.30
  7.2 57.6 %all-gather.3.cloned.1.call-start = ((), (), s32[]{:S(2)}) async-start(), calls=%async_computation.4 | async-start | bytes 1966080 | tf_op jit(solution)/shard_map/all_gather | solution.py:45
  9.1 119.2 %copy-start.1 = (f32[256,768]{1,0:T(8,128)}, f32[256,768]{1,0:T(8,128)S(1)}, u32[]{:S(2)}) copy-start(f32[256,768]{1,0:T(8,128)S(1)} %get-tuple-element.334) | copy-start | bytes 2359300
  9.1 1.3 copy-start.37
  10.3 117.9 %reduce-scatter.5.cloned.1.call-start = ((), (), s32[]{:S(2)}) async-start(), calls=%async_computation.5 | async-start | bytes 1966080 | tf_op jit(solution)/shard_map/reduce_scatter | solution.py:53
  10.4 54.4 %copy-start.34 = (f32[2,192]{1,0:T(2,128)S(1)}, f32[2,192]{1,0:T(2,128)}, u32[]{:S(2)}) copy-start(f32[2,192]{1,0:T(2,128)} %param.33) | copy-start | bytes 4612
  73.9 2.4 copy-start.24
  73.9 2.4 copy-start.26
  87.0 2.9 copy-start.10
  87.0 41.2 %copy-start.31 = (f32[768]{0:T(1024)S(1)}, f32[768]{0:T(1024)}, u32[]{:S(2)}) copy-start(f32[768]{0:T(1024)} %param.35) | copy-start | bytes 9220
  89.9 39.8 %copy-start.27 = (f32[768]{0:T(1024)S(1)}, f32[768]{0:T(1024)}, u32[]{:S(2)}) copy-start(f32[768]{0:T(1024)} %param.42) | copy-start | bytes 9220
  89.9 39.8 %copy-start.32 = (f32[768]{0:T(1024)S(1)}, f32[768]{0:T(1024)}, u32[]{:S(2)}) copy-start(f32[768]{0:T(1024)} %param.43) | copy-start | bytes 9220
  89.9 95.1 %all-gather.5.cloned.1.call-start = ((), (), s32[]{:S(2)}) async-start(), calls=%async_computation.6 | async-start | bytes 1966080 | tf_op jit(solution)/shard_map/all_gather | solution.py:45
  130.7 97.9 %reduce-scatter.9.cloned.1.call-start = ((), (), s32[]{:S(2)}) async-start(), calls=%async_computation.8 | async-start | bytes 1966080 | tf_op jit(solution)/shard_map/reduce_scatter | solution.py:59
  130.7 16.6 %collective-permute-start = (bf16[256,768]{1,0:T(8,128)(2,1)S(1)}, bf16[256,768]{1,0:T(8,128)(2,1)S(1)}, u32[]{:S(2)}, u32[]{:S(2)}) collective-permute-start(bf16[256,768]{1,0:T(8,128)(2,1)S(1)} %copy-done.15), channel_id=1, source_target_pairs={{0,1},{1,2},{2,3},{3,0},{4,5},{5,6},{6,7},{7,4},{8,9},{9,10},{10,1... | collective-permute-start | bytes 1179656 | tf_op jit(solution)/shard_map/ppermute | solution.py:17
  130.9 39.4 %collective-permute-start.1 = (bf16[256,768]{1,0:T(8,128)(2,1)S(1)}, bf16[256,768]{1,0:T(8,128)(2,1)S(1)}, u32[]{:S(2)}, u32[]{:S(2)}) collective-permute-start(bf16[256,768]{1,0:T(8,128)(2,1)S(1)} %copy-done.15), channel_id=1, source_target_pairs={{0,3},{1,0},{2,1},{3,2},{4,7},{5,4},{6,5},{7,6},{8,11},{9,8},{10,9... | collective-permute-start | bytes 1179656 | tf_op jit(solution)/shard_map/ppermute | solution.py:20
  147.3 32.3 %collective-permute-start.2 = (bf16[256,768]{1,0:T(8,128)(2,1)S(1)}, bf16[256,768]{1,0:T(8,128)(2,1)}, u32[]{:S(2)}, u32[]{:S(2)}) collective-permute-start(bf16[256,768]{1,0:T(8,128)(2,1)S(1)} %collective-permute-done), channel_id=1, source_target_pairs={{0,1},{1,2},{2,3},{3,0},{4,5},{5,6},{6,7},{7,4},{8,9},{9,10},{10,1... | collective-permute-start | bytes 1179656 | tf_op jit(solution)/shard_map/ppermute | solution.py:17
  163.2 21.8 %copy-start.35 = (f32[192]{0:T(256)S(1)}, f32[192]{0:T(256)}, u32[]{:S(2)}) copy-start(f32[192]{0:T(256)} %param.39) | copy-start | bytes 2308
  187.1 4.7 copy-start.18
  191.8 1.8 copy-start.16
  193.6 71.4 %reduce-scatter.7.cloned.1.call-start = ((), (), s32[]{:S(2)}) async-start(), calls=%async_computation.7 | async-start | bytes 1966080 | tf_op jit(solution)/shard_map/reduce_scatter | solution.py:53
  194.9 3.0 copy-start.12
  197.8 67.2 %copy-start.33 = (f32[768]{0:T(1024)S(1)}, f32[768]{0:T(1024)}, u32[]{:S(2)}) copy-start(f32[768]{0:T(1024)} %param.41) | copy-start | bytes 9220
  197.9 165.1 %reduce-scatter.11.cloned.1.call-start = ((), (), s32[]{:S(2)}) async-start(), calls=%async_computation.9 | async-start | bytes 1966080 | tf_op jit(solution)/shard_map/reduce_scatter | solution.py:59
  267.4 2.1 copy-start.3
  269.6 29.9 %copy-start.25 = (bf16[192,768]{1,0:T(8,128)(2,1)S(1)}, bf16[192,768]{1,0:T(8,128)(2,1)}, u32[]{:S(2)}) copy-start(bf16[192,768]{1,0:T(8,128)(2,1)} %param.34) | copy-start | bytes 884740
  269.6 13.8 %collective-permute-start.3 = (bf16[256,768]{1,0:T(8,128)(2,1)S(1)}, bf16[256,768]{1,0:T(8,128)(2,1)S(1)}, u32[]{:S(2)}, u32[]{:S(2)}) collective-permute-start(bf16[256,768]{1,0:T(8,128)(2,1)S(1)} %get-tuple-element.314), channel_id=1, source_target_pairs={{0,1},{1,2},{2,3},{3,0},{4,5},{5,6},{6,7},{7,4},{8,9},{9,10},{10,1... | collective-permute-start | bytes 1179656 | tf_op jit(solution)/shard_map/ppermute | solution.py:17
  269.7 18.9 %collective-permute-start.4 = (bf16[256,768]{1,0:T(8,128)(2,1)S(1)}, bf16[256,768]{1,0:T(8,128)(2,1)S(1)}, u32[]{:S(2)}, u32[]{:S(2)}) collective-permute-start(bf16[256,768]{1,0:T(8,128)(2,1)S(1)} %get-tuple-element.314), channel_id=1, source_target_pairs={{0,3},{1,0},{2,1},{3,2},{4,7},{5,4},{6,5},{7,6},{8,11},{9,8},{10,9... | collective-permute-start | bytes 1179656 | tf_op jit(solution)/shard_map/ppermute | solution.py:20
  283.4 15.4 %collective-permute-start.5 = (bf16[256,768]{1,0:T(8,128)(2,1)S(1)}, bf16[256,768]{1,0:T(8,128)(2,1)S(1)}, u32[]{:S(2)}, u32[]{:S(2)}) collective-permute-start(bf16[256,768]{1,0:T(8,128)(2,1)S(1)} %collective-permute-done.3), channel_id=1, source_target_pairs={{0,1},{1,2},{2,3},{3,0},{4,5},{5,6},{6,7},{7,4},{8,9},{9,10},{10,1... | collective-permute-start | bytes 1179656 | tf_op jit(solution)/shard_map/ppermute | solution.py:17
  301.6 2.3 copy-start.6
  312.2 2.3 copy-start.6
  329.2 3.7 copy-start.5
  329.2 3.7 copy-start.17
  329.2 162.5 %all-reduce.8.cloned.1.call-start = ((), (), s32[]{:S(2)}) async-start(), calls=%async_computation.11 | async-start | bytes 7077888 | tf_op jit(solution)/shard_map/psum | solution.py:295
  332.9 4.1 copy-start.36
  334.2 2.8 copy-start.20
  339.3 23.7 %copy-start.2 = (f32[256,768]{1,0:T(8,128)S(1)}, f32[256,768]{1,0:T(8,128)}, u32[]{:S(2)}) copy-start(f32[256,768]{1,0:T(8,128)} %copy-done.1) | copy-start | bytes 2359300
  339.3 25.1 %copy-start.4 = (f32[256,768]{1,0:T(8,128)S(1)}, f32[256,768]{1,0:T(8,128)}, u32[]{:S(2)}) copy-start(f32[256,768]{1,0:T(8,128)} %copy-done.3) | copy-start | bytes 2359300
  339.3 240.0 %all-reduce.6.cloned.1.call-start = ((), (), s32[]{:S(2)}) async-start(), calls=%async_computation.10 | async-start | bytes 3145728 | tf_op jit(solution)/shard_map/psum | solution.py:315
  364.4 1.3 copy-start.29
  365.7 2.3 copy-start.9
  368.0 58.5 %copy-start.8 = (bf16[2,512,3,192]{1,3,2,0:T(8,128)(2,1)S(1)}, bf16[2,512,3,192]{1,3,2,0:T(8,128)(2,1)}, u32[]{:S(2)}) copy-start(bf16[2,512,3,192]{1,3,2,0:T(8,128)(2,1)} %get-tuple-element.159) | copy-start | bytes 3538948
  579.3 2.9 copy-start.23
  579.3 3.7 copy-start.22
  582.2 1.6 copy-start.21
  582.2 2.5 copy-start.14
  (6 other events, 6.8 us)
Sparse Core Ops, SparseCore 0:
  10.4 39.8 all-gather.2
  90.0 38.1 reduce-scatter.4
  130.8 54.2 all-gather.4
  193.7 34.8 reduce-scatter.8
  230.7 34.2 reduce-scatter.6
  329.3 33.5 reduce-scatter.10
  367.8 72.8 all-reduce.7
  446.5 132.7 all-reduce.5
